TPU v7x, 32 devices: a whole 2x2x4 slice. The times are simulated.
32 devices in a mesh: traj: 4 (over y, x), grid: 8 (over z, core).
Axes of the slice: x: 2, y: 2, z: 4, core: 2. Of those that a mesh axis runs over, the one named last changes fastest.
Arguments:
- psi_modes: float32 [4, 2, 256, 256, 256], P('traj', None, None, 'grid'), may hold values from -6 to 6
- noise: float32 [4, 2, 256, 256, 256], P('traj', None, 'grid'), may hold values from -6 to 6
- mask: int32 [256, 256, 256], P(None, 'grid'), may hold values from 0 to 1, as said below
Outputs:
- psi_next: float32 [4, 2, 256, 256, 256], P('traj', None, None, 'grid')
- momentum_hist: float32 [128], replicated
Inputs may be any that keep to these rules, and one draw needn't show every extreme that they name: mask is 0 at every mode whose signed third index has magnitude 256/4 or more, and 1 at some mode whose signed third index has magnitude 256/4 - 1.
All inputs are finite; a program needn't handle non-finite values.
Results may differ from a plain program's by a relative error of at most 0.00023.
Values sent between devices are 32-bit elements; how exact they have to be, the bound alone decides.
A program may use at most 192 MiB of HBM per device.

v0:
```python
import jax
import jax.numpy as jnp
from jax import lax
from jax.sharding import PartitionSpec as P

SHELLS = 128


time_step = 1.0
damping = 0.05
coupling = 10.0
chem_potential = 1.0
noise_amp = 0.1
trap_strength = 8.0
hist_blocks = 8


def signed_of(index, count):
    return jnp.where(index < count // 2, index, index - count)


def dft_table(out_index, in_index, count, sign):
    phase = (out_index[:, None] * in_index[None, :] % count).astype(jnp.float32) * (
        2.0 * jnp.pi / count
    )
    scale = 1.0 / jnp.sqrt(jnp.float32(count))
    return (jnp.cos(phase) * scale, sign * jnp.sin(phase) * scale)


def transform(pair, letter, tables):
    layout = "txyz"
    target = layout.replace(letter, "k")
    pattern = "k" + letter + "," + layout + "->" + target
    cos_tab, sin_tab = tables

    def contract(table, values):
        return jnp.einsum(pattern, table, values, precision=lax.Precision.HIGHEST)

    real_part, imag_part = pair
    new_real = contract(cos_tab, real_part) - contract(sin_tab, imag_part)
    new_imag = contract(sin_tab, real_part) + contract(cos_tab, imag_part)
    return (new_real, new_imag)


def shell_sums(occupation, shells):
    flat_occ = occupation.reshape(hist_blocks, -1)
    flat_shell = shells.reshape(hist_blocks, -1)
    shell_ids = jnp.arange(SHELLS, dtype=jnp.int32)

    def add_block(running, pieces):
        block_occ, block_shell = pieces
        hits = jnp.where(
            block_shell[:, None] == shell_ids[None, :], block_occ[:, None], jnp.float32(0.0)
        )
        return (running + jnp.sum(hits, axis=0), None)

    result, _ = lax.scan(add_block, jnp.zeros((SHELLS,), jnp.float32), (flat_occ, flat_shell))
    return result


def shards(psi_modes, noise, mask):
    grid_rank = lax.axis_index("grid")
    extent_x = mask.shape[0]
    extent_y = noise.shape[3]
    extent_z = mask.shape[2]
    rows_local = mask.shape[1]
    planes_local = noise.shape[2]
    quarter = extent_z // 4
    all_cols = jnp.arange(extent_z, dtype=jnp.int32)
    column_ids = jnp.concatenate([all_cols[:quarter], all_cols[extent_z - quarter :]])

    def select_cols(values):
        return jnp.concatenate([values[..., :quarter], values[..., extent_z - quarter :]], axis=-1)

    index_x = jnp.arange(extent_x, dtype=jnp.int32)
    index_y = jnp.arange(extent_y, dtype=jnp.int32)
    modes_x = signed_of(index_x, extent_x)
    modes_y = signed_of(grid_rank * rows_local + jnp.arange(rows_local, dtype=jnp.int32), extent_y)
    modes_z = signed_of(column_ids, extent_z)
    wave_x = modes_x.astype(jnp.float32) * (2.0 * jnp.pi / extent_x)
    wave_y = modes_y.astype(jnp.float32) * (2.0 * jnp.pi / extent_y)
    wave_z = modes_z.astype(jnp.float32) * (2.0 * jnp.pi / extent_z)
    ksq = wave_x[:, None, None] ** 2 + wave_y[None, :, None] ** 2 + wave_z[None, None, :] ** 2
    theta = 0.25 * time_step * ksq
    magnitude = jnp.exp(-damping * theta) * select_cols(mask).astype(jnp.float32)
    fac_real = magnitude * jnp.cos(theta)
    fac_imag = -magnitude * jnp.sin(theta)
    start_real = select_cols(psi_modes[:, 0])
    start_imag = select_cols(psi_modes[:, 1])
    kicked = (
        start_real * fac_real - start_imag * fac_imag,
        start_real * fac_imag + start_imag * fac_real,
    )
    inverse_x = dft_table(index_x, index_x, extent_x, 1.0)
    inverse_y = dft_table(index_y, index_y, extent_y, 1.0)
    inverse_z = dft_table(all_cols, column_ids, extent_z, 1.0)
    forward_x = dft_table(index_x, index_x, extent_x, -1.0)
    forward_y = dft_table(index_y, index_y, extent_y, -1.0)
    forward_z = dft_table(column_ids, all_cols, extent_z, -1.0)
    partial_value = transform(kicked, "x", inverse_x)
    spaced = transform(
        (
            lax.all_to_all(partial_value[0], "grid", split_axis=1, concat_axis=2, tiled=True),
            lax.all_to_all(partial_value[1], "grid", split_axis=1, concat_axis=2, tiled=True),
        ),
        "y",
        inverse_y,
    )
    field_real, field_imag = transform(spaced, "z", inverse_z)
    pos_x = (grid_rank * planes_local + jnp.arange(planes_local, dtype=jnp.int32)).astype(
        jnp.float32
    )
    pos_x = (pos_x + 0.5) / extent_x - 0.5
    pos_y = (index_y.astype(jnp.float32) + 0.5) / extent_y - 0.5
    pos_z = (all_cols.astype(jnp.float32) + 0.5) / extent_z - 0.5
    potential = trap_strength * (
        pos_x[:, None, None] ** 2 + pos_y[None, :, None] ** 2 + pos_z[None, None, :] ** 2
    )
    density = field_real * field_real + field_imag * field_imag
    energy = potential + coupling * density - chem_potential
    decay = jnp.exp(-damping * energy * time_step)
    evo_real = decay * jnp.cos(energy * time_step)
    evo_imag = -decay * jnp.sin(energy * time_step)
    moved_real = field_real * evo_real - field_imag * evo_imag + noise_amp * noise[:, 0]
    moved_imag = field_real * evo_imag + field_imag * evo_real + noise_amp * noise[:, 1]
    partial_fwd = transform((moved_real, moved_imag), "z", forward_z)
    partial_fwd = transform(partial_fwd, "y", forward_y)
    final_real, final_imag = transform(
        (
            lax.all_to_all(partial_fwd[0], "grid", split_axis=2, concat_axis=1, tiled=True),
            lax.all_to_all(partial_fwd[1], "grid", split_axis=2, concat_axis=1, tiled=True),
        ),
        "x",
        forward_x,
    )
    out_real = final_real * fac_real - final_imag * fac_imag
    out_imag = final_real * fac_imag + final_imag * fac_real
    occupation = jnp.sum(out_real * out_real + out_imag * out_imag, axis=0)
    radius_sq = (
        modes_x[:, None, None] ** 2 + modes_y[None, :, None] ** 2 + modes_z[None, None, :] ** 2
    )
    shells = jnp.minimum(radius_sq * SHELLS // (2 * quarter * quarter), SHELLS - 1).astype(
        jnp.int32
    )
    local_hist = shell_sums(occupation, shells)
    group_hist = lax.psum(local_hist, "grid")
    total_hist = lax.psum(group_hist, "traj")
    traj_count = psi_modes.shape[0] * lax.axis_size("traj")
    momentum_hist = total_hist * (SHELLS / (traj_count * extent_x * extent_y * extent_z))
    filler = jnp.zeros(out_real.shape[:-1] + (extent_z - 2 * quarter,), jnp.float32)
    out_real = jnp.concatenate([out_real[..., :quarter], filler, out_real[..., quarter:]], axis=-1)
    out_imag = jnp.concatenate([out_imag[..., :quarter], filler, out_imag[..., quarter:]], axis=-1)
    psi_next = jnp.stack([out_real, out_imag], axis=1)
    return (psi_next, momentum_hist)


def solution(mesh):
    placed = (
        P("traj", None, None, "grid", None),
        P("traj", None, "grid", None, None),
        P(None, "grid", None),
    )
    return jax.shard_map(
        shards,
        mesh=mesh,
        in_specs=placed,
        out_specs=(P("traj", None, None, "grid", None), P()),
        check_vma=False,
    )
```

profile of v0, /device:TPU:0, one launch (start us, length us, event | category | flops | bytes accessed | tf_op | source)
XLA Modules:
  0.0 1121.3 jit_solution(12711466431174675706)
XLA Ops:
  0.8 11.0 fusion.246
  11.8 9.9 copy.140
  21.8 9.9 copy.143
  31.7 7.9 fusion.247
  43.1 4.6 copy.142
  52.0 17.0 %multiply_add_fusion.1 = (f32[256,32,128]{0,2,1:T(8,128)S(1)}, f32[256,32,128]{0,2,1:T(8,128)S(1)}) fusion(f32[256,32,64]{0,2,1:T(8,128)S(1)} %get-tuple-element.71, f32[256,32,64]{0,2,1:T(8,128)S(1)} %get-tuple-element.70, f32[256,32,64]{0,2,1:T(8,128)S(1)} %get-tuple-element.80, f32[256,32,64]{0,2,1:T(8,128)S(1)} %get-tuple-element.81, ...), kind=kLoop, calls=%fused_computation.63 | loop fusion | flops 17825792 | bytes 21004800 | tf_op jit(solution)/shard_map/add | solution.py:92
  73.5 6.9 subtract_bitcast_fusion.1
  80.4 5.5 copy.97
  85.9 6.6 all-to-all-start
  92.6 7.4 fusion.40
  100.0 6.9 add_bitcast_fusion.1
  106.9 5.5 copy.100
  112.4 74.2 %all-to-all-done = f32[1,256,32,128]{3,2,0,1:T(8,128)} async-done(((f32[1,256,32,128]{3,2,0,1:T(8,128)}), f32[1,256,32,128]{3,2,0,1:T(8,128)}, u32[]{:S(2)}, u32[]{:S(2)}) %all-to-all-start) | async-done | bytes 4194336 | tf_op jit(solution)/shard_map/all_to_all | solution.py:103
  186.6 5.0 all-to-all-start.1
  195.0 9.9 fusion.51
  204.9 10.1 fusion.37
  214.9 70.6 %all-to-all-done.1 = f32[1,256,32,128]{3,2,0,1:T(8,128)} async-done(((f32[1,256,32,128]{3,2,0,1:T(8,128)}), f32[1,256,32,128]{3,2,0,1:T(8,128)}, u32[]{:S(2)}, u32[]{:S(2)}) %all-to-all-start.1) | async-done | bytes 4194336 | tf_op jit(solution)/shard_map/all_to_all | solution.py:104
  289.0 7.5 convolution_add_fusion.2
  296.5 7.5 fusion.21
  304.0 10.3 fusion.19
  314.4 8.0 convolution_subtract_fusion.2
  322.4 9.9 fusion.25
  332.3 60.2 %bitcast_add_fusion = (f32[32,256,256]{2,1,0:T(8,128)S(1)}, f32[32,256,256]{2,1,0:T(8,128)S(1)}) fusion(f32[1,2,32,256,256]{4,3,2,1,0:T(8,128)} %param.6, f32[256]{0:T(256)S(1)} %add_multiply_fusion.5, f32[32,256]{1,0:T(8,128)S(1)} %broadcast_add_fusion.1, f32[32,256,256]{2,1,0:T(8,128)} %fusion.19, f32[32,256,256]{2,1,0:T(8,128)} %fusion.25, ...), kind=kOutput, calls=%fused_computation.10 | convolution fusion | flops 3271557120 | bytes 63079424 | tf_op jit(solution)/shard_map/kz,txyz->txyk/dot_general | solution.py:37
  392.5 7.2 fusion.72
  399.8 7.5 fusion.76
  407.2 7.2 convolution_add_fusion.1
  414.5 7.7 convolution_subtract_fusion.1
  422.2 8.2 fusion.47
  430.5 10.5 subtract_bitcast_fusion
  441.0 5.5 copy.111
  446.4 4.6 all-to-all-start.2
  454.9 4.9 mul.604
  459.8 10.3 fusion.34
  470.2 9.9 add_bitcast_fusion
  480.1 5.5 copy.117
  485.6 59.4 %all-to-all-done.2 = f32[1,32,256,128]{3,1,0,2:T(8,128)} async-done(((f32[1,32,256,128]{3,1,0,2:T(8,128)}), f32[1,32,256,128]{3,1,0,2:T(8,128)}, u32[]{:S(2)}, u32[]{:S(2)}) %all-to-all-start.2) | async-done | bytes 4194336 | tf_op jit(solution)/shard_map/all_to_all | solution.py:130
  545.0 5.0 all-to-all-start.3
  550.0 6.7 fusion.16
  557.7 4.6 copy.112
  565.0 5.2 copy.114
  570.3 8.8 fusion.45
  579.0 7.1 fusion.31
  586.1 57.9 %all-to-all-done.3 = f32[1,32,256,128]{3,1,0,2:T(8,128)} async-done(((f32[1,32,256,128]{3,1,0,2:T(8,128)}), f32[1,32,256,128]{3,1,0,2:T(8,128)}, u32[]{:S(2)}, u32[]{:S(2)}) %all-to-all-start.3) | async-done | bytes 4194336 | tf_op jit(solution)/shard_map/all_to_all | solution.py:131
  644.0 4.6 copy.118
  651.2 5.3 copy.120
  656.5 8.0 convolution_subtract_fusion
  664.6 24.0 %multiply_add_fusion = (f32[1,256,32,128]{1,3,2,0:T(8,128)}, f32[1,256,32,128]{1,3,2,0:T(8,128)S(1)}, f32[1,256,32,128]{1,3,2,0:T(8,128)}) fusion(s32[1,256,32,64]{1,3,2,0:T(8,128)S(1)} %bitcast.199, s32[1,256,32,64]{1,3,2,0:T(8,128)S(1)} %bitcast.198, f32[128]{0:T(128)S(1)} %multiply_multiply_fusion.1, f32[256,32]{0,1:T(8,128)S(1)} %broadcast_add_fusion.2, ...), kind=kOutput, calls=%fused_computation.56 | convolution fusion | flops 3241148416 | bytes 29655552 | tf_op jit(solution)/shard_map/kx,txyz->tkyz/dot_general | solution.py:37
  690.3 5.5 copy.123
  704.3 5.6 copy.125
  714.4 5.5 copy.127
  719.8 4.9 reshape.508
  724.8 357.3 %while.11 = (s32[]{:T(128)}, f32[128]{0:T(128)S(1)}, s32[8,131072]{1,0:T(8,128)}, f32[8,131072]{1,0:T(8,128)}, s32[]{:T(128)}, /*index=5*/s32[]{:T(128)}) while((s32[]{:T(128)}, f32[128]{0:T(128)S(1)}, s32[8,131072]{1,0:T(8,128)}, f32[8,131072]{1,0:T(8,128)}, s32[]{:T(128)}, /*index=5*/s32[]{:T(128)}) %tuple.43), condition=%wide.region_2.3_spmd.clone, body=%wide.region_0.2_spmd.clone.sunk | while | flops 50331776 | bytes 3147863 | solution.py:57
  729.9 39.5 %select_reduce_fusion.2 = f32[128]{0:T(128)S(1)} fusion(f32[131072]{0:T(1024)S(1)} %bitcast.192, s32[131072]{0:T(1024)S(1)} %bitcast.193), kind=kLoop, calls=%fused_computation.2.clone.1 | loop fusion | flops 50331520 | bytes 1049088 | tf_op jit(solution)/shard_map/while/body/eval_jaxpr/reduce_sum | solution.py:55
  774.6 39.5 %select_reduce_fusion.2 = f32[128]{0:T(128)S(1)} fusion(f32[131072]{0:T(1024)S(1)} %bitcast.192, s32[131072]{0:T(1024)S(1)} %bitcast.193), kind=kLoop, calls=%fused_computation.2.clone.1 | loop fusion | flops 50331520 | bytes 1049088 | tf_op jit(solution)/shard_map/while/body/eval_jaxpr/reduce_sum | solution.py:55
  819.2 39.5 %select_reduce_fusion.2 = f32[128]{0:T(128)S(1)} fusion(f32[131072]{0:T(1024)S(1)} %bitcast.192, s32[131072]{0:T(1024)S(1)} %bitcast.193), kind=kLoop, calls=%fused_computation.2.clone.1 | loop fusion | flops 50331520 | bytes 1049088 | tf_op jit(solution)/shard_map/while/body/eval_jaxpr/reduce_sum | solution.py:55
  863.9 39.5 %select_reduce_fusion.2 = f32[128]{0:T(128)S(1)} fusion(f32[131072]{0:T(1024)S(1)} %bitcast.192, s32[131072]{0:T(1024)S(1)} %bitcast.193), kind=kLoop, calls=%fused_computation.2.clone.1 | loop fusion | flops 50331520 | bytes 1049088 | tf_op jit(solution)/shard_map/while/body/eval_jaxpr/reduce_sum | solution.py:55
  908.5 39.5 %select_reduce_fusion.2 = f32[128]{0:T(128)S(1)} fusion(f32[131072]{0:T(1024)S(1)} %bitcast.192, s32[131072]{0:T(1024)S(1)} %bitcast.193), kind=kLoop, calls=%fused_computation.2.clone.1 | loop fusion | flops 50331520 | bytes 1049088 | tf_op jit(solution)/shard_map/while/body/eval_jaxpr/reduce_sum | solution.py:55
  953.2 39.5 %select_reduce_fusion.2 = f32[128]{0:T(128)S(1)} fusion(f32[131072]{0:T(1024)S(1)} %bitcast.192, s32[131072]{0:T(1024)S(1)} %bitcast.193), kind=kLoop, calls=%fused_computation.2.clone.1 | loop fusion | flops 50331520 | bytes 1049088 | tf_op jit(solution)/shard_map/while/body/eval_jaxpr/reduce_sum | solution.py:55
  997.9 39.5 %select_reduce_fusion.2 = f32[128]{0:T(128)S(1)} fusion(f32[131072]{0:T(1024)S(1)} %bitcast.192, s32[131072]{0:T(1024)S(1)} %bitcast.193), kind=kLoop, calls=%fused_computation.2.clone.1 | loop fusion | flops 50331520 | bytes 1049088 | tf_op jit(solution)/shard_map/while/body/eval_jaxpr/reduce_sum | solution.py:55
  1042.5 39.5 %select_reduce_fusion.2 = f32[128]{0:T(128)S(1)} fusion(f32[131072]{0:T(1024)S(1)} %bitcast.192, s32[131072]{0:T(1024)S(1)} %bitcast.193), kind=kLoop, calls=%fused_computation.2.clone.1 | loop fusion | flops 50331520 | bytes 1049088 | tf_op jit(solution)/shard_map/while/body/eval_jaxpr/reduce_sum | solution.py:55
  1082.1 14.5 %psum.14 = f32[128]{0:T(128)S(1)} all-reduce(f32[128]{0:T(128)S(1)} %get-tuple-element.29), channel_id=1, replica_groups=mesh['traj'=4,'grid'=8] {'grid'}, use_global_device_ids=true, to_apply=%region_3.4 | all-reduce | flops 128 | bytes 1024 | tf_op jit(solution)/shard_map/psum | solution.py:146
  1096.6 9.9 psum.15
  1107.0 7.8 maximum_bitcast_fusion
  1114.8 6.3 pad_maximum_fusion
  (82 shorter events, 85.7 us)
Async XLA Ops:
  47.7 4.3 copy-start.8
  69.0 4.4 copy-start.7
  69.0 4.4 copy-start.4
  85.9 100.6 %all-to-all-start = ((f32[1,256,32,128]{3,2,0,1:T(8,128)}), f32[1,256,32,128]{3,2,0,1:T(8,128)}, u32[]{:S(2)}, u32[]{:S(2)}) async-start(f32[1,256,32,128]{3,2,0,1:T(8,128)} %copy.97), calls=%async_computation | async-start | bytes 8388608 | tf_op jit(solution)/shard_map/all_to_all | solution.py:103
  92.6 7.4 copy-start.5
  186.6 98.9 %all-to-all-start.1 = ((f32[1,256,32,128]{3,2,0,1:T(8,128)}), f32[1,256,32,128]{3,2,0,1:T(8,128)}, u32[]{:S(2)}, u32[]{:S(2)}) async-start(f32[1,256,32,128]{3,2,0,1:T(8,128)} %copy.100), calls=%async_computation.1 | async-start | bytes 8388608 | tf_op jit(solution)/shard_map/all_to_all | solution.py:104
  285.5 3.4 copy-start.12
  304.0 10.4 copy-start.11
  414.5 16.0 %copy-start = (f32[32,256,128]{2,1,0:T(8,128)}, f32[32,256,128]{2,1,0:T(8,128)S(1)}, u32[]{:S(2)}) copy-start(f32[32,256,128]{2,1,0:T(8,128)S(1)} %convolution_add_fusion.1) | copy-start | bytes 12582916
  422.2 8.2 copy-start.3
  446.4 98.5 %all-to-all-start.2 = ((f32[1,32,256,128]{3,1,0,2:T(8,128)}), f32[1,32,256,128]{3,1,0,2:T(8,128)}, u32[]{:S(2)}, u32[]{:S(2)}) async-start(f32[1,32,256,128]{3,1,0,2:T(8,128)} %copy.111), calls=%async_computation.2 | async-start | bytes 8388608 | tf_op jit(solution)/shard_map/all_to_all | solution.py:130
  459.8 10.4 copy-start.1
  545.0 99.0 %all-to-all-start.3 = ((f32[1,32,256,128]{3,1,0,2:T(8,128)}), f32[1,32,256,128]{3,1,0,2:T(8,128)}, u32[]{:S(2)}, u32[]{:S(2)}) async-start(f32[1,32,256,128]{3,1,0,2:T(8,128)} %copy.117), calls=%async_computation.3 | async-start | bytes 8388608 | tf_op jit(solution)/shard_map/all_to_all | solution.py:131
  570.3 8.8 copy-start.6
  656.5 8.0 copy-start.2
  656.5 8.0 copy-start.9
  656.5 8.1 copy-start.10
where the time goes:
time: 1130 us; the launch traced here: 1120 us
  other arithmetic  360 us (32%)
  matrix products  266 us (24%)
  waiting for transfers between devices  262 us (23%)
  local copies, waits for them, and re-layouts  186 us (16%)
  blocking collectives  24.4 us (2%)
  starting transfers between devices  21.2 us (2%)
    reduce_sum x8, other arithmetic, add_block(): return (running + jnp.sum(hits, axis=0), None)  316 us
    dot_general x24, matrix products, contract(): return jnp.einsum(pattern, table, values, precision=lax.Precision.HIGHEST)  266 us
    all_to_all x1, waiting for transfers between devices, shards(): lax.all_to_all(partial_value[0], 'grid', split_axis=1, concat_axis=2, til...  74.2 us
    all_to_all x1, waiting for transfers between devices, shards(): lax.all_to_all(partial_value[1], 'grid', split_axis=1, concat_axis=2, til...  70.6 us
    all_to_all x1, waiting for transfers between devices, shards(): lax.all_to_all(partial_fwd[0], 'grid', split_axis=2, concat_axis=1, tiled...  59.4 us
    all_to_all x1, waiting for transfers between devices, shards(): lax.all_to_all(partial_fwd[1], 'grid', split_axis=2, concat_axis=1, tiled...  57.9 us
    dynamic_slice x16, local copies, waits for them, and re-layouts, shell_sums(): lax.scan(add_block, jnp.zeros((SHELLS,), jnp.float32), (flat_occ, flat_sh...  40.9 us
    unnamed x30, local copies, waits for them, and re-layouts  28.5 us
  transfers between devices with their start and end apart: 4, of which 4 were waited for; matrix products, arithmetic and copies ran while one was open for 10% of the time, Pallas kernels for 0%

commit v1 on v0

v1 whole, which is shorter than its diff:
```python
import jax
import jax.numpy as jnp
from jax import lax
from jax.sharding import PartitionSpec as P

SHELLS = 128


time_step = 1.0
damping = 0.05
coupling = 10.0
chem_potential = 1.0
noise_amp = 0.1
trap_strength = 8.0
max_chunks = 4


def signed_of(index, count):
    return jnp.where(index < count // 2, index, index - count)


def dft_table(out_index, in_index, count, sign):
    phase = (out_index[:, None] * in_index[None, :] % count).astype(jnp.float32) * (
        2.0 * jnp.pi / count
    )
    scale = 1.0 / jnp.sqrt(jnp.float32(count))
    return (jnp.cos(phase) * scale, sign * jnp.sin(phase) * scale)


def axis_factor(modes, count):
    wave = modes.astype(jnp.float32) * (2.0 * jnp.pi / count)
    theta = 0.25 * time_step * wave * wave
    size = jnp.exp(-damping * theta)
    return (size * jnp.cos(theta), -size * jnp.sin(theta))


def scaled(table, factor, dim):
    real, imag = factor
    if dim == 0:
        real, imag = real[:, None], imag[:, None]
    else:
        real, imag = real[None, :], imag[None, :]
    return (table[0] * real - table[1] * imag, table[0] * imag + table[1] * real)


def block_table(table):
    real, imag = table
    top = jnp.stack([real, -imag], axis=1)
    bottom = jnp.stack([imag, real], axis=1)
    return jnp.stack([top, bottom], axis=0)


def contract(pattern, table, values):
    return jnp.einsum(pattern, table, values, precision=lax.Precision.HIGH)


def cos_sin(angle):
    turns = jnp.round(angle * (2.0 / jnp.pi))
    rest = angle - turns * 1.5703125
    rest = rest - turns * 4.837512969970703125e-4
    rest = rest - turns * 7.54978995489188216e-8
    sq = rest * rest
    sine = rest + rest * sq * (
        -1.6666654611e-1 + sq * (8.3321608736e-3 + sq * -1.9515295891e-4)
    )
    cosine = 1.0 + sq * (
        -0.5 + sq * (4.166664568298827e-2 + sq * (-1.388731625493765e-3 + sq * 2.443315711809948e-5))
    )
    quadrant = turns.astype(jnp.int32)
    odd = (quadrant & 1) != 0
    cos_out = jnp.where(odd, sine, cosine)
    sin_out = jnp.where(odd, cosine, sine)
    cos_out = jnp.where(((quadrant + 1) & 2) != 0, -cos_out, cos_out)
    sin_out = jnp.where((quadrant & 2) != 0, -sin_out, sin_out)
    return cos_out, sin_out


def shell_sums(occupation, modes_x, modes_y, modes_z, limit):
    base = (modes_x[:, None] ** 2 + modes_y[None, :] ** 2) * SHELLS
    row_shell = jnp.minimum(base // limit, SHELLS - 1).reshape(-1)
    row_rest = (base % limit).reshape(-1)
    col = modes_z**2 * SHELLS
    col_shell = col // limit
    col_rest = col % limit
    flat = occupation.reshape(row_rest.shape[0], -1)
    carry = row_rest[:, None] + col_rest[None, :] >= limit
    zero = jnp.float32(0.0)
    both = jnp.concatenate([jnp.where(carry, zero, flat), jnp.where(carry, flat, zero)], axis=-1)
    shell_ids = jnp.arange(SHELLS, dtype=jnp.int32)
    hits = (row_shell[None, :] == shell_ids[:, None]).astype(jnp.float32)
    sums = jnp.einsum("sr,rc->sc", hits, both, precision=lax.Precision.HIGHEST)
    offset = jnp.concatenate([col_shell, col_shell + 1])
    shell = jnp.minimum(shell_ids[:, None] + offset[None, :], SHELLS - 1)
    picked = jnp.where(shell[None] == shell_ids[:, None, None], sums[None], zero)
    return jnp.sum(picked, axis=(1, 2))


def shards(psi_modes, noise, mask):
    grid_rank = lax.axis_index("grid")
    ranks = lax.axis_size("grid")
    extent_x = mask.shape[0]
    extent_y = noise.shape[3]
    extent_z = mask.shape[2]
    rows_local = mask.shape[1]
    planes_local = noise.shape[2]
    quarter = extent_z // 4
    chunks = max_chunks
    while planes_local % chunks:
        chunks -= 1
    depth = planes_local // chunks

    def select_cols(values):
        return jnp.concatenate([values[..., :quarter], values[..., extent_z - quarter :]], axis=-1)

    index_x, index_y, all_cols = lax.optimization_barrier(
        tuple(jnp.arange(extent, dtype=jnp.int32) for extent in (extent_x, extent_y, extent_z))
    )
    column_ids = select_cols(all_cols)
    modes_x = signed_of(index_x, extent_x)
    modes_y_all = signed_of(index_y, extent_y)
    modes_y = signed_of(grid_rank * rows_local + jnp.arange(rows_local, dtype=jnp.int32), extent_y)
    modes_z = signed_of(column_ids, extent_z)
    fac_x = axis_factor(modes_x, extent_x)
    fac_y = axis_factor(modes_y_all, extent_y)
    fac_z = axis_factor(modes_z, extent_z)
    inverse_x = block_table(scaled(dft_table(index_x, index_x, extent_x, 1.0), fac_x, 1))
    inverse_y = block_table(scaled(dft_table(index_y, index_y, extent_y, 1.0), fac_y, 1))
    inverse_z = block_table(scaled(dft_table(all_cols, column_ids, extent_z, 1.0), fac_z, 1))
    forward_x = block_table(scaled(dft_table(index_x, index_x, extent_x, -1.0), fac_x, 0))
    forward_y = block_table(scaled(dft_table(index_y, index_y, extent_y, -1.0), fac_y, 0))
    forward_z = block_table(scaled(dft_table(column_ids, all_cols, extent_z, -1.0), fac_z, 0))
    inverse_x = inverse_x.reshape(2, ranks, chunks, depth, 2, extent_x)
    inverse_y = inverse_y.reshape(2, extent_y, 2, ranks, rows_local)
    forward_y = forward_y.reshape(2, ranks, rows_local, 2, extent_y)
    forward_x = forward_x.reshape(2, extent_x, 2, ranks, chunks, depth)

    kept = select_cols(mask).astype(jnp.float32)
    start = select_cols(psi_modes) * kept
    pos_x = (grid_rank * planes_local + jnp.arange(planes_local, dtype=jnp.int32)).astype(
        jnp.float32
    )
    pos_x = (pos_x + 0.5) / extent_x - 0.5
    pos_y = (index_y.astype(jnp.float32) + 0.5) / extent_y - 0.5
    pos_z = (all_cols.astype(jnp.float32) + 0.5) / extent_z - 0.5

    def exchange(values):
        return lax.all_to_all(values, "grid", split_axis=2, concat_axis=2, tiled=True)

    arrived = [
        exchange(contract("dgpcx,tcxyz->tdgpyz", inverse_x[:, :, chunk], start))
        for chunk in range(chunks)
    ]
    final = None
    for chunk in range(chunks):
        low = chunk * depth
        spaced = contract("ekdsy,tdspyz->tepkz", inverse_y, arrived[chunk])
        field = contract("ekdz,tdpyz->tepyk", inverse_z, spaced)
        field_real, field_imag = field[:, 0], field[:, 1]
        potential = trap_strength * (
            pos_x[low : low + depth, None, None] ** 2
            + pos_y[None, :, None] ** 2
            + pos_z[None, None, :] ** 2
        )
        density = field_real * field_real + field_imag * field_imag
        energy = potential + coupling * density - chem_potential
        decay = jnp.exp(-damping * energy * time_step)
        cosine, sine = cos_sin(jnp.minimum(energy * time_step, 4096.0))
        evo_real = decay * cosine
        evo_imag = -decay * sine
        kick = noise_amp * noise[:, :, low : low + depth]
        moved = jnp.stack(
            [
                field_real * evo_real - field_imag * evo_imag + kick[:, 0],
                field_real * evo_imag + field_imag * evo_real + kick[:, 1],
            ],
            axis=1,
        )
        partial_fwd = contract("ekdz,tdpyz->tepyk", forward_z, moved)
        partial_fwd = contract("egkdy,tdpyz->tegpkz", forward_y, partial_fwd)
        returned = exchange(partial_fwd)
        piece = contract("ekdsp,tdspyz->tekyz", forward_x[:, :, :, :, chunk], returned)
        final = piece if final is None else final + piece
    out = final * kept
    occupation = jnp.sum(out * out, axis=(0, 1))
    local_hist = shell_sums(occupation, modes_x, modes_y, modes_z, 2 * quarter * quarter)
    total_hist = lax.psum(local_hist, ("traj", "grid"))
    traj_count = psi_modes.shape[0] * lax.axis_size("traj")
    momentum_hist = total_hist * (SHELLS / (traj_count * extent_x * extent_y * extent_z))
    filler = jnp.zeros(out.shape[:-1] + (extent_z - 2 * quarter,), jnp.float32)
    psi_next = jnp.concatenate([out[..., :quarter], filler, out[..., quarter:]], axis=-1)
    return (psi_next, momentum_hist)


def solution(mesh):
    placed = (
        P("traj", None, None, "grid", None),
        P("traj", None, "grid", None, None),
        P(None, "grid", None),
    )
    return jax.shard_map(
        shards,
        mesh=mesh,
        in_specs=placed,
        out_specs=(P("traj", None, None, "grid", None), P()),
        check_vma=False,
    )
```

time: 1130 us -> 582 us (0.52)
  other arithmetic: 360 us -> 69.2 us
  matrix products: 266 us -> 131 us
  local copies, waits for them, and re-layouts: 186 us -> 77.7 us
  waiting for transfers between devices: 262 us -> 220 us
  starting transfers between devices: 21.2 us -> 36.5 us
  blocking collectives: 24.4 us -> 38 us
    reduce_sum x8 -> x1, other arithmetic: 316 us -> 1.89 us  [shell_sums(): return jnp.sum(picked, axis=(1, 2))]
    dot_general x24 -> x25, matrix products: 266 us -> 131 us  [the longest x24 128 us: contract(): return jnp.einsum(pattern, table, values, precision=lax.Precision.HIGH)]
    all_to_all x4 -> x8, waiting for transfers between devices: 262 us -> 220 us  [exchange(): lax.all_to_all(values, 'grid', split_axis=2, concat_axis=2, tiled=True)]
    dynamic_slice x16 -> x0, local copies, waits for them, and re-layouts: 40.9 us -> none  [shell_sums(): lax.scan(add_block, jnp.zeros((SHELLS,), jnp.float32), (flat_occ, flat_sh...]
    unnamed x30 -> x42, local copies, waits for them, and re-layouts: 28.5 us -> 1.47 us
    all_to_all x6 -> x0, local copies, waits for them, and re-layouts: 20.3 us -> none  [the longest x2 7.26 us: shards(): lax.all_to_all(partial_fwd[0], 'grid', split_axis=2, concat_axis=1, tiled...]
    add x3 -> x0, local copies, waits for them, and re-layouts: 16.5 us -> none  [the longest x2 11 us: transform(): new_imag = contract(sin_tab, real_part) + contract(cos_tab, imag_part)]
    all_to_all x4 -> x8, starting transfers between devices: 21.2 us -> 36.5 us  [exchange(): lax.all_to_all(values, 'grid', split_axis=2, concat_axis=2, tiled=True)]
  transfers between devices with their start and end apart: 4 -> 8, of which waited for: 4 -> 8; matrix products, arithmetic and copies ran while one was open for 10% -> 30% of each run, Pallas kernels for 0% -> 0%
where the time goes in v1:
time: 582 us; the launch traced here: 574 us
  waiting for transfers between devices  220 us (38%)
  matrix products  131 us (23%)
  local copies, waits for them, and re-layouts  77.7 us (13%)
  other arithmetic  69.2 us (12%)
  blocking collectives  38 us (7%)
  starting transfers between devices  36.5 us (6%)
    all_to_all x8, waiting for transfers between devices, exchange(): lax.all_to_all(values, 'grid', split_axis=2, concat_axis=2, tiled=True)  220 us
    dot_general x24, matrix products, contract(): return jnp.einsum(pattern, table, values, precision=lax.Precision.HIGH)  128 us
    psum x1, blocking collectives, shards(): total_hist = lax.psum(local_hist, ('traj', 'grid'))  38 us
    all_to_all x8, starting transfers between devices, exchange(): lax.all_to_all(values, 'grid', split_axis=2, concat_axis=2, tiled=True)  36.5 us
    add x2, other arithmetic, shards(): field_real * evo_real - field_imag * evo_imag + kick[:, 0]  20.2 us
    slice x2, local copies, waits for them, and re-layouts, shards(): out[..., :quarter]  17.1 us
    transpose x8, local copies, waits for them, and re-layouts, contract(): return jnp.einsum(pattern, table, values, precision=lax.Precision.HIGH)  14.1 us
    concatenate x1, other arithmetic, shards(): jnp.concatenate([out[..., :quarter], filler, out[..., quarter:]], axis=-1)  13 us
  transfers between devices with their start and end apart: 8, of which 8 were waited for; matrix products, arithmetic and copies ran while one was open for 30% of the time, Pallas kernels for 0%

profile of v1, /device:TPU:0, one launch (start us, length us, event | category | flops | bytes accessed | tf_op | source)
XLA Modules:
  0.0 574.4 jit_solution(2185708760382104908)
XLA Ops:
  0.8 4.9 fusion.186
  5.8 9.4 %slice_bitcast_fusion.1 = (f32[2,256,32,64]{3,2,1,0:T(8,128)S(1)}, f32[2,256,32,64]{3,2,1,0:T(8,128)}) fusion(f32[1,2,256,32,256]{4,3,2,1,0:T(8,128)} %param.3), kind=kLoop, calls=%fused_computation.15 | loop fusion | bytes 16777216 | tf_op jit(solution)/shard_map/concatenate | solution.py:113
  17.5 5.5 fusion
  23.1 7.0 %fusion.104 = f32[1,2,8,8,32,128]{5,3,2,1,4,0:T(8,128)S(1)} fusion(f32[2,256,32,128,1,1]{3,2,1,0,5,4:T(8,128)S(1)} %fusion, f32[2,8,4,8,2,256]{5,3,4,1,0,2:T(8,128)S(1)} %maximum_maximum_fusion), kind=kOutput, calls=%fused_computation.202 | convolution fusion | flops 1610612736 | bytes 10747904 | tf_op jit(solution)/shard_map/dgpcx,tcxyz->tdgpyz/dot_general | solution.py:54
  30.1 1.6 copy.131
  31.7 6.6 %all-to-all-start.2 = ((f32[1,2,8,8,32,128]{5,3,1,4,0,2:T(8,128)}), f32[1,2,8,8,32,128]{5,3,1,4,0,2:T(8,128)S(1)}, u32[]{:S(2)}, u32[]{:S(2)}) async-start(f32[1,2,8,8,32,128]{5,3,1,4,0,2:T(8,128)} %copy.131), calls=%async_computation.2 | async-start | bytes 4194304 | tf_op jit(solution)/shard_map/all_to_all | solution.py:147
  38.3 9.9 %fusion.101 = f32[1,2,8,8,32,128]{5,3,2,1,4,0:T(8,128)S(1)} fusion(f32[2,256,32,128,1,1]{3,2,1,0,5,4:T(8,128)} %copy-done, f32[2,8,4,8,2,256]{5,3,4,1,0,2:T(8,128)S(1)} %maximum_maximum_fusion), kind=kOutput, calls=%fused_computation.201 | convolution fusion | flops 1610612736 | bytes 10747904 | tf_op jit(solution)/shard_map/dgpcx,tcxyz->tdgpyz/dot_general | solution.py:54
  49.8 37.5 %all-to-all-done.2 = f32[1,2,8,8,32,128]{5,3,1,4,0,2:T(8,128)S(1)} async-done(((f32[1,2,8,8,32,128]{5,3,1,4,0,2:T(8,128)}), f32[1,2,8,8,32,128]{5,3,1,4,0,2:T(8,128)S(1)}, u32[]{:S(2)}, u32[]{:S(2)}) %all-to-all-start.2) | async-done | bytes 2097184 | tf_op jit(solution)/shard_map/all_to_all | solution.py:147
  88.6 4.7 all-to-all-start
  93.4 9.9 %fusion.110 = f32[1,2,8,8,32,128]{5,3,2,1,4,0:T(8,128)S(1)} fusion(f32[2,256,32,128,1,1]{3,2,1,0,5,4:T(8,128)} %copy-done, f32[2,8,4,8,2,256]{5,3,4,1,0,2:T(8,128)S(1)} %maximum_maximum_fusion), kind=kOutput, calls=%fused_computation.204 | convolution fusion | flops 1610612736 | bytes 10747904 | tf_op jit(solution)/shard_map/dgpcx,tcxyz->tdgpyz/dot_general | solution.py:54
  105.1 11.4 %fusion.107 = f32[1,2,8,8,32,128]{5,3,2,1,4,0:T(8,128)} fusion(f32[2,256,32,128,1,1]{3,2,1,0,5,4:T(8,128)} %copy-done, f32[2,8,4,8,2,256]{5,3,4,1,0,2:T(8,128)S(1)} %maximum_maximum_fusion), kind=kOutput, calls=%fused_computation.203 | convolution fusion | flops 1610612736 | bytes 10747904 | tf_op jit(solution)/shard_map/dgpcx,tcxyz->tdgpyz/dot_general | solution.py:54
  116.5 25.5 %all-to-all-done = f32[1,2,8,8,32,128]{5,3,1,4,0,2:T(8,128)} async-done(((f32[1,2,8,8,32,128]{5,3,1,4,0,2:T(8,128)}), f32[1,2,8,8,32,128]{5,3,1,4,0,2:T(8,128)}, u32[]{:S(2)}, u32[]{:S(2)}) %all-to-all-start) | async-done | bytes 2097184 | tf_op jit(solution)/shard_map/all_to_all | solution.py:147
  142.0 3.6 all-to-all-start.6
  146.1 3.2 copy.138
  152.3 1.9 fusion.155
  155.4 10.1 %fusion.184 = (f32[1,2,8,256,256]{4,3,2,1,0:T(8,128)}, f32[1,2,8,256,256]{4,3,2,1,0:T(8,128)}, f32[1,2,8,256,256]{4,3,2,1,0:T(8,128)S(1)}, f32[1,2,8,256,256]{4,3,2,1,0:T(8,128)S(1)}) fusion(f32[1,2,32,256,256]{4,3,2,1,0:T(8,128)} %param.4), kind=kLoop, calls=%fused_computation.386 | loop fusion | bytes 33554432 | tf_op jit(solution)/shard_map/slice | solution.py:170
  165.5 4.0 copy_multiply_fusion.2
  169.5 25.1 %all-to-all-done.6 = f32[1,2,8,8,32,128]{5,3,1,4,0,2:T(8,128)S(1)} async-done(((f32[1,2,8,8,32,128]{5,3,1,4,0,2:T(8,128)}), f32[1,2,8,8,32,128]{5,3,1,4,0,2:T(8,128)S(1)}, u32[]{:S(2)}, u32[]{:S(2)}) %all-to-all-start.6) | async-done | bytes 2097184 | tf_op jit(solution)/shard_map/all_to_all | solution.py:147
  194.6 4.3 all-to-all-start.4
  199.0 4.1 fusion.84
  203.1 4.1 fusion.90
  207.2 3.6 convolution_bitcast_fusion.2
  210.8 3.6 convolution_bitcast_fusion.3
  214.4 10.2 %slice_add_fusion.7 = (f32[1,1,8,256,256]{4,3,1,2,0:T(8,128)S(1)}, f32[1,1,8,256,256]{4,3,1,2,0:T(8,128)S(1)}, f32[1,1,8,256,256]{4,3,1,2,0:T(8,128)}, f32[1,1,8,256,256]{4,3,1,2,0:T(8,128)}) fusion(f32[1,2,8,256,256]{4,3,1,2,0:T(8,128)S(1)} %copy-done.5, f32[1,2,8,256,256]{4,3,1,2,0:T(8,128)S(1)} %convolution_bitcast_fusion.3, ...), kind=kLoop, calls=%fused_computation.136 | loop fusion | flops 61865984 | bytes 25183232 | tf_op jit(solution)/shard_map/add | solution.py:173
  224.6 1.9 fusion.13
  226.5 1.9 fusion.113
  228.4 1.6 copy.127
  230.0 18.0 %all-to-all-done.4 = f32[1,2,8,8,32,128]{5,3,1,4,0,2:T(8,128)} async-done(((f32[1,2,8,8,32,128]{5,3,1,4,0,2:T(8,128)}), f32[1,2,8,8,32,128]{5,3,1,4,0,2:T(8,128)}, u32[]{:S(2)}, u32[]{:S(2)}) %all-to-all-start.4) | async-done | bytes 2097184 | tf_op jit(solution)/shard_map/all_to_all | solution.py:147
  248.0 4.3 all-to-all-start.1
  252.4 8.0 %copy_multiply_fusion = (f32[1,2,8,256,256]{4,3,1,2,0:T(8,128)}, f32[1,2,8,256,256]{4,3,1,2,0:T(8,128)}) fusion(f32[1,2,8,256,256]{4,3,2,1,0:T(8,128)} %get-tuple-element.22, f32[1,2,8,256,256]{4,3,2,1,0:T(8,128)} %get-tuple-element.23), kind=kLoop, calls=%fused_computation.41 | loop fusion | flops 2097152 | bytes 16777216 | tf_op jit(solution)/shard_map/mul | solution.py:170
  260.4 1.9 fusion.16
  262.3 1.9 fusion.116
  264.2 1.6 copy.135
  265.8 35.6 %all-to-all-done.1 = f32[1,2,8,8,32,128]{5,4,1,3,0,2:T(8,128)} async-done(((f32[1,2,8,8,32,128]{5,4,1,3,0,2:T(8,128)}), f32[1,2,8,8,32,128]{5,4,1,3,0,2:T(8,128)}, u32[]{:S(2)}, u32[]{:S(2)}) %all-to-all-start.1) | async-done | bytes 2097184 | tf_op jit(solution)/shard_map/all_to_all | solution.py:147
  301.4 4.5 all-to-all-start.3
  305.9 3.5 fusion.72
  309.4 4.1 fusion.78
  313.5 3.6 convolution_bitcast_fusion
  317.1 3.6 convolution_bitcast_fusion.1
  320.8 10.0 %slice_add_fusion.1 = (f32[1,1,8,256,256]{4,3,1,2,0:T(8,128)}, f32[1,1,8,256,256]{4,3,1,2,0:T(8,128)}, f32[1,1,8,256,256]{4,3,1,2,0:T(8,128)S(1)}, f32[1,1,8,256,256]{4,3,1,2,0:T(8,128)S(1)}) fusion(f32[1,2,8,256,256]{4,3,1,2,0:T(8,128)S(1)} %copy-done.2, f32[1,2,8,256,256]{4,3,1,2,0:T(8,128)S(1)} %convolution_bitcast_fusion, ...), kind=kLoop, calls=%fused_computation.130 | loop fusion | flops 61865984 | bytes 25183232 | tf_op jit(solution)/shard_map/add | solution.py:173
  330.8 1.9 fusion.19
  332.7 1.9 fusion.119
  336.1 18.9 %all-to-all-done.3 = f32[1,2,8,8,32,128]{5,4,1,3,0,2:T(8,128)} async-done(((f32[1,2,8,8,32,128]{5,4,1,3,0,2:T(8,128)}), f32[1,2,8,8,32,128]{5,4,1,3,0,2:T(8,128)}, u32[]{:S(2)}, u32[]{:S(2)}) %all-to-all-start.3) | async-done | bytes 2097184 | tf_op jit(solution)/shard_map/all_to_all | solution.py:147
  354.9 3.6 all-to-all-start.5
  358.6 3.7 fusion.22
  362.2 1.9 fusion.122
  364.1 1.6 copy.149
  365.7 41.8 %all-to-all-done.5 = f32[1,2,8,8,32,128]{5,4,1,3,0,2:T(8,128)S(1)} async-done(((f32[1,2,8,8,32,128]{5,4,1,3,0,2:T(8,128)}), f32[1,2,8,8,32,128]{5,4,1,3,0,2:T(8,128)S(1)}, u32[]{:S(2)}, u32[]{:S(2)}) %all-to-all-start.5) | async-done | bytes 2097184 | tf_op jit(solution)/shard_map/all_to_all | solution.py:147
  407.5 4.8 all-to-all-start.7
  412.4 5.3 copy.151
  419.3 8.8 %fusion.86 = f32[32,128,2,256,1,1]{3,1,5,4,2,0:T(8,128)} fusion(f32[1,2,8,8,32,128]{5,4,1,3,0,2:T(8,128)} %all-to-all-done.1, f32[2,256,2,8,4,8]{1,3,5,2,0,4:T(8,128)S(1)} %maximum_maximum_fusion.1), kind=kOutput, calls=%fused_computation.158 | convolution fusion | flops 1610612736 | bytes 10747904 | tf_op jit(solution)/shard_map/ekdsp,tdspyz->tekyz/dot_general | solution.py:54
  428.1 8.8 %fusion.80 = f32[32,128,2,256,1,1]{3,1,5,4,2,0:T(8,128)} fusion(f32[1,2,8,8,32,128]{5,4,1,3,0,2:T(8,128)} %all-to-all-done.3, f32[2,256,2,8,4,8]{1,3,5,2,0,4:T(8,128)S(1)} %maximum_maximum_fusion.1), kind=kOutput, calls=%fused_computation.152 | convolution fusion | flops 1610612736 | bytes 10747904 | tf_op jit(solution)/shard_map/ekdsp,tdspyz->tekyz/dot_general | solution.py:54
  436.9 6.8 %fusion.74 = f32[32,128,2,256,1,1]{3,1,5,4,2,0:T(8,128)} fusion(f32[1,2,8,8,32,128]{5,4,1,3,0,2:T(8,128)S(1)} %all-to-all-done.5, f32[2,256,2,8,4,8]{1,3,5,2,0,4:T(8,128)S(1)} %maximum_maximum_fusion.1), kind=kOutput, calls=%fused_computation.146 | convolution fusion | flops 1610612736 | bytes 10747904 | tf_op jit(solution)/shard_map/ekdsp,tdspyz->tekyz/dot_general | solution.py:54
  443.7 17.6 %all-to-all-done.7 = f32[1,2,8,8,32,128]{5,4,1,3,0,2:T(8,128)} async-done(((f32[1,2,8,8,32,128]{5,4,1,3,0,2:T(8,128)}), f32[1,2,8,8,32,128]{5,4,1,3,0,2:T(8,128)}, u32[]{:S(2)}, u32[]{:S(2)}) %all-to-all-start.7) | async-done | bytes 2097184 | tf_op jit(solution)/shard_map/all_to_all | solution.py:147
  461.3 18.4 %multiply_reduce_fusion = (f32[256,32,128]{0,2,1:T(8,128)}, f32[1,2,256,32,128]{2,4,1,3,0:T(8,128)}) fusion(f32[256,32,128]{0,2,1:T(8,128)} %copy.151, f32[2,256,2,8,4,8]{1,3,5,2,0,4:T(8,128)S(1)} %maximum_maximum_fusion.1, f32[1,2,8,8,32,128]{5,4,1,3,0,2:T(8,128)} %all-to-all-done.7, f32[32,128,2,256,1,1]{3,1,5,4,2,0:T(8,128)} %fusion.74, ...), kind=kOutput, calls=%fused_computation.13 | convolution fusion | flops 1622147072 | bytes 44302336 | tf_op jit(solution)/shard_map/ekdsp,tdspyz->tekyz/dot_general | solution.py:54
  479.7 5.5 copy.154
  485.2 5.9 %bitcast_select_fusion.1 = (f32[8192,128]{1,0:T(8,128)S(1)}, f32[8192,128]{1,0:T(8,128)S(1)}) fusion(f32[256,32,128]{2,1,0:T(8,128)} %copy.154, s32[128]{0:T(128)S(1)} %and_select_fusion, s32[8192]{0:T(1024)S(1)} %get-tuple-element.47), kind=kLoop, calls=%fused_computation.46 | loop fusion | flops 4194304 | bytes 12616192 | tf_op jit(solution)/shard_map/jit(_where)/select_n | solution.py:88
  491.0 3.4 fusion.1
  494.5 1.9 select_reduce_fusion
  496.4 38.0 %psum.7 = f32[128]{0:T(128)S(1)} all-reduce(f32[128]{0:T(128)S(1)} %select_reduce_fusion), channel_id=1, replica_groups=mesh['traj'=4,'grid'=8] {'traj','grid'}, use_global_device_ids=true, to_apply=%region_2.3 | all-reduce | flops 128 | bytes 1024 | tf_op jit(solution)/shard_map/psum | solution.py:186
  534.9 7.8 %fusion.185 = (f32[1,2,256,32,64]{2,4,1,3,0:T(8,128)}, f32[1,2,256,32,64]{2,4,1,3,0:T(8,128)}) fusion(f32[1,2,256,32,128]{2,4,1,3,0:T(8,128)} %get-tuple-element.89), kind=kLoop, calls=%fused_computation.387 | loop fusion | bytes 16777216 | tf_op jit(solution)/shard_map/slice | solution.py:190
  542.7 9.2 %copy.152 = f32[1,2,256,32,64]{4,3,2,1,0:T(8,128)} copy(f32[1,2,256,32,64]{2,4,1,3,0:T(8,128)} %get-tuple-element.36) | data formatting | bytes 8388608 | tf_op jit(solution)/shard_map/slice | solution.py:190
  552.0 9.2 %copy.153 = f32[1,2,256,32,64]{4,3,2,1,0:T(8,128)} copy(f32[1,2,256,32,64]{2,4,1,3,0:T(8,128)} %get-tuple-element.37) | data formatting | bytes 8388608 | tf_op jit(solution)/shard_map/slice | solution.py:190
  561.1 13.0 %pad_maximum_fusion = f32[1,2,256,32,256]{4,3,2,1,0:T(8,128)} fusion(f32[1,2,256,32,64]{4,3,2,1,0:T(8,128)} %copy.153, f32[1,2,256,32,64]{4,3,2,1,0:T(8,128)} %copy.152, f32[256]{0:T(256)S(1)} %pad.5.clone), kind=kLoop, calls=%fused_computation | loop fusion | flops 8388608 | bytes 25166848 | tf_op jit(solution)/shard_map/concatenate | solution.py:190
  (87 shorter events, 15.7 us)
Async XLA Ops:
  16.3 6.8 %copy-start.1 = (f32[256,32,128]{2,1,0:T(8,128)}, f32[256,32,128]{2,1,0:T(8,128)S(1)}, u32[]{:S(2)}) copy-start(f32[256,32,128]{2,1,0:T(8,128)S(1)} %add_convert_fusion) | copy-start | bytes 12582916
  23.1 7.0 %copy-start = (f32[2,256,32,128,1,1]{3,2,1,0,5,4:T(8,128)}, f32[2,256,32,128,1,1]{3,2,1,0,5,4:T(8,128)S(1)}, u32[]{:S(2)}) copy-start(f32[2,256,32,128,1,1]{3,2,1,0,5,4:T(8,128)S(1)} %fusion) | copy-start | bytes 25165828
  31.7 55.6 %all-to-all-start.2 = ((f32[1,2,8,8,32,128]{5,3,1,4,0,2:T(8,128)}), f32[1,2,8,8,32,128]{5,3,1,4,0,2:T(8,128)S(1)}, u32[]{:S(2)}, u32[]{:S(2)}) async-start(f32[1,2,8,8,32,128]{5,3,1,4,0,2:T(8,128)} %copy.131), calls=%async_computation.2 | async-start | bytes 4194304 | tf_op jit(solution)/shard_map/all_to_all | solution.py:147
  87.3 1.4 copy-start.6
  88.6 53.4 %all-to-all-start = ((f32[1,2,8,8,32,128]{5,3,1,4,0,2:T(8,128)}), f32[1,2,8,8,32,128]{5,3,1,4,0,2:T(8,128)}, u32[]{:S(2)}, u32[]{:S(2)}) async-start(f32[1,2,8,8,32,128]{5,3,1,4,0,2:T(8,128)} %copy.123), calls=%async_computation | async-start | bytes 4194304 | tf_op jit(solution)/shard_map/all_to_all | solution.py:147
  142.0 52.6 %all-to-all-start.6 = ((f32[1,2,8,8,32,128]{5,3,1,4,0,2:T(8,128)}), f32[1,2,8,8,32,128]{5,3,1,4,0,2:T(8,128)S(1)}, u32[]{:S(2)}, u32[]{:S(2)}) async-start(f32[1,2,8,8,32,128]{5,3,1,4,0,2:T(8,128)} %copy.145), calls=%async_computation.6 | async-start | bytes 4194304 | tf_op jit(solution)/shard_map/all_to_all | solution.py:147
  194.6 53.4 %all-to-all-start.4 = ((f32[1,2,8,8,32,128]{5,3,1,4,0,2:T(8,128)}), f32[1,2,8,8,32,128]{5,3,1,4,0,2:T(8,128)}, u32[]{:S(2)}, u32[]{:S(2)}) async-start(f32[1,2,8,8,32,128]{5,3,1,4,0,2:T(8,128)} %copy.138), calls=%async_computation.4 | async-start | bytes 4194304 | tf_op jit(solution)/shard_map/all_to_all | solution.py:147
  198.9 4.1 copy-start.9
  203.1 4.1 copy-start.17
  203.1 4.1 copy-start.19
  207.2 7.2 %copy-start.5 = (f32[1,2,8,256,256]{4,3,1,2,0:T(8,128)S(1)}, f32[1,2,8,256,256]{4,3,1,2,0:T(8,128)}, u32[]{:S(2)}) copy-start(f32[1,2,8,256,256]{4,3,1,2,0:T(8,128)} %get-tuple-element.96) | copy-start | bytes 12582916
  210.8 3.6 copy-start.4
  214.4 10.2 %copy-start.11 = (f32[1,128,2,256]{3,1,2,0:T(8,128)S(1)}, f32[1,128,2,256]{3,1,2,0:T(8,128)}, u32[]{:S(2)}) copy-start(f32[1,128,2,256]{3,1,2,0:T(8,128)} %get-tuple-element.42) | copy-start | bytes 786436
  214.4 10.2 %copy-start.14 = (f32[1,128,2,256]{3,1,2,0:T(8,128)S(1)}, f32[1,128,2,256]{3,1,2,0:T(8,128)}, u32[]{:S(2)}) copy-start(f32[1,128,2,256]{3,1,2,0:T(8,128)} %get-tuple-element.43) | copy-start | bytes 786436
  248.0 53.4 %all-to-all-start.1 = ((f32[1,2,8,8,32,128]{5,4,1,3,0,2:T(8,128)}), f32[1,2,8,8,32,128]{5,4,1,3,0,2:T(8,128)}, u32[]{:S(2)}, u32[]{:S(2)}) async-start(f32[1,2,8,8,32,128]{5,4,1,3,0,2:T(8,128)} %copy.127), calls=%async_computation.1 | async-start | bytes 4194304 | tf_op jit(solution)/shard_map/all_to_all | solution.py:147
  252.3 8.1 %copy-start.7 = (f32[1,1,8,256,256]{4,3,1,2,0:T(8,128)S(1)}, f32[1,1,8,256,256]{4,3,1,2,0:T(8,128)}, u32[]{:S(2)}) copy-start(f32[1,1,8,256,256]{4,3,1,2,0:T(8,128)} %get-tuple-element.72) | copy-start | bytes 6291460
  252.3 8.1 %copy-start.8 = (f32[1,1,8,256,256]{4,3,1,2,0:T(8,128)S(1)}, f32[1,1,8,256,256]{4,3,1,2,0:T(8,128)}, u32[]{:S(2)}) copy-start(f32[1,1,8,256,256]{4,3,1,2,0:T(8,128)} %get-tuple-element.73) | copy-start | bytes 6291460
  252.4 8.1 %copy-start.12 = (f32[1,128,2,256]{3,1,2,0:T(8,128)S(1)}, f32[1,128,2,256]{3,1,2,0:T(8,128)}, u32[]{:S(2)}) copy-start(f32[1,128,2,256]{3,1,2,0:T(8,128)} %get-tuple-element.42) | copy-start | bytes 786436
  252.4 8.1 %copy-start.15 = (f32[1,128,2,256]{3,1,2,0:T(8,128)S(1)}, f32[1,128,2,256]{3,1,2,0:T(8,128)}, u32[]{:S(2)}) copy-start(f32[1,128,2,256]{3,1,2,0:T(8,128)} %get-tuple-element.43) | copy-start | bytes 786436
  301.4 53.6 %all-to-all-start.3 = ((f32[1,2,8,8,32,128]{5,4,1,3,0,2:T(8,128)}), f32[1,2,8,8,32,128]{5,4,1,3,0,2:T(8,128)}, u32[]{:S(2)}, u32[]{:S(2)}) async-start(f32[1,2,8,8,32,128]{5,4,1,3,0,2:T(8,128)} %copy.135), calls=%async_computation.3 | async-start | bytes 4194304 | tf_op jit(solution)/shard_map/all_to_all | solution.py:147
  305.9 3.5 copy-start.10
  309.4 4.1 copy-start.18
  309.4 4.1 copy-start.20
  313.5 7.2 %copy-start.3 = (f32[1,2,8,256,256]{4,3,1,2,0:T(8,128)S(1)}, f32[1,2,8,256,256]{4,3,1,2,0:T(8,128)}, u32[]{:S(2)}) copy-start(f32[1,2,8,256,256]{4,3,1,2,0:T(8,128)} %get-tuple-element.94) | copy-start | bytes 12582916
  317.1 3.6 copy-start.2
  320.8 10.0 %copy-start.13 = (f32[1,128,2,256]{3,1,2,0:T(8,128)S(1)}, f32[1,128,2,256]{3,1,2,0:T(8,128)}, u32[]{:S(2)}) copy-start(f32[1,128,2,256]{3,1,2,0:T(8,128)} %get-tuple-element.42) | copy-start | bytes 786436
  320.8 10.0 %copy-start.16 = (f32[1,128,2,256]{3,1,2,0:T(8,128)S(1)}, f32[1,128,2,256]{3,1,2,0:T(8,128)}, u32[]{:S(2)}) copy-start(f32[1,128,2,256]{3,1,2,0:T(8,128)} %get-tuple-element.43) | copy-start | bytes 786436
  354.9 52.6 %all-to-all-start.5 = ((f32[1,2,8,8,32,128]{5,4,1,3,0,2:T(8,128)}), f32[1,2,8,8,32,128]{5,4,1,3,0,2:T(8,128)S(1)}, u32[]{:S(2)}, u32[]{:S(2)}) async-start(f32[1,2,8,8,32,128]{5,4,1,3,0,2:T(8,128)} %copy.142), calls=%async_computation.5 | async-start | bytes 4194304 | tf_op jit(solution)/shard_map/all_to_all | solution.py:147
  407.5 53.8 %all-to-all-start.7 = ((f32[1,2,8,8,32,128]{5,4,1,3,0,2:T(8,128)}), f32[1,2,8,8,32,128]{5,4,1,3,0,2:T(8,128)}, u32[]{:S(2)}, u32[]{:S(2)}) async-start(f32[1,2,8,8,32,128]{5,4,1,3,0,2:T(8,128)} %copy.149), calls=%async_computation.7 | async-start | bytes 4194304 | tf_op jit(solution)/shard_map/all_to_all | solution.py:147
